TPU v7x, 256 devices: a whole 4x4x8 slice. The times are simulated.
256 devices in a mesh: req: 32 (over x, z), mdl: 8 (over y, core).
Axes of the slice: x: 4, y: 4, z: 8, core: 2. Of those that a mesh axis runs over, the one named last changes fastest.
Arguments:
- hidden_state: bfloat16 [1024, 2880], P('req'), may hold values from -6 to 6
- cached_length_list: int32 [1024], P('req'), may hold values from 1 to 2047, as said below
- page_table: int32 [1024, 16], P('req'), may hold values from 0 to 5631, as said below
- paged_cache_store: bfloat16 [5632, 128, 1024], P('req', None, 'mdl'), may hold values from -68 to 68, as said below
- attention_gain: float32 [2880], replicated, may hold values from 0.5 to 1.5
- qkv_weight: bfloat16 [2880, 5120], P('req', 'mdl'), may hold values from -0.109375 to 0.109375
- qkv_bias: float32 [5120], P('mdl'), may hold values from -3 to 3
- sink_logit_values: float32 [64], P('mdl'), may hold values from -1 to 4
- output_weight: bfloat16 [4096, 2880], P('mdl', 'req'), may hold values from -0.25 to 0.25
- output_bias: float32 [2880], replicated, may hold values from -3 to 3
- expert_gain: float32 [2880], replicated, may hold values from 0.5 to 1.5
- router_weight: bfloat16 [2880, 32], replicated, may hold values from -0.109375 to 0.109375
- router_bias: float32 [32], replicated, may hold values from -4 to 4
- expert_routes: int32 [1024, 4], P('req'), may hold values from 0 to 31, all different within a row; in each aligned block of 32 rows (0 to 31, 32 to 63, ...) at most 8 rows name the same one
- expand_weight: bfloat16 [32, 2880, 5760], P('req', None, 'mdl'), may hold values from -0.109375 to 0.109375
- expand_bias: float32 [32, 5760], P('req', 'mdl'), may hold values from -10 to 10
- reduce_weight: bfloat16 [32, 2880, 2880], P('req', 'mdl'), may hold values from -0.109375 to 0.109375
- reduce_bias: float32 [32, 2880], replicated, may hold values from -3 to 3
Outputs:
- layer_output: bfloat16 [1024, 2880], P('req', 'mdl')
Inputs may be any that keep to these rules, and one draw needn't show every extreme that they name: `cached_length_list`: requests r and r + 1 within a block of 32 requests share an owner; about one request in eight holds between 1536 and 2047 cached positions, at most 8 of each owner's 32, and the others at most 256; some owner, and the last owner, hold exactly 8 long ones. `page_table`: the entries of request r name pages of its owner's block, pages r // 32 * 176 to that plus 176 - 1; the pages that hold cached positions differ between requests; entries past a request's last used page are to be ignored. `paged_cache_store`: keys are stored rotated at their own positions. `expert_routes`: each token names 4 different experts; of the rows of one index of req no expert is named by more than 8.
All inputs are finite; a program needn't handle non-finite values.
Results may differ from a plain program's by a relative error of at most 0.024.
Values may be sent and summed in bfloat16 or wider, within the bound.
A program may use at most 192 MiB of HBM per device.

v0:
```python
import math
import jax
import jax.numpy as jnp
from jax import lax
from jax.sharding import PartitionSpec as P

HEAD_SIZE = 64
PAGE_POSITIONS = 128
SHORT_MAX = 256
QUERY_PER_KEY = 8
SHORT_PAGES = 2
norm_epsilon = 1e-05
rope_theta = 150000.0
swiglu_limit = 7.0
swiglu_alpha = 1.702


def normalize(row_values, gain):
    value_rows = row_values.astype(jnp.float32)
    mean_square = jnp.mean(value_rows * value_rows, axis=-1, keepdims=True)
    return value_rows * lax.rsqrt(mean_square + norm_epsilon) * gain


def apply_rotation(value_rows, positions):
    half_width = value_rows.shape[-1] // 2
    exponent = jnp.arange(half_width, dtype=jnp.float32) * (2.0 / value_rows.shape[-1])
    frequency = jnp.power(rope_theta, -exponent)
    angles = positions.astype(jnp.float32)[:, None] * frequency[None, :]
    cosine = jnp.cos(angles)[:, None, :]
    sine_part = jnp.sin(angles)[:, None, :]
    first_half = value_rows[..., :half_width]
    second_half = value_rows[..., half_width:]
    return jnp.concatenate(
        [
            first_half * cosine - second_half * sine_part,
            second_half * cosine + first_half * sine_part,
        ],
        axis=-1,
    )


def head_identity(kv_heads):
    return (jnp.arange(kv_heads)[:, None] == jnp.arange(kv_heads)[None, :]).astype(jnp.float32)


def spread_queries(query_rows):
    row_count, kv_heads, group_size, head_width = query_rows.shape
    key_slot = (jnp.arange(2) == 0).astype(jnp.float32)
    turned = jnp.swapaxes(query_rows, 2, 3).astype(jnp.float32)
    spread = jnp.einsum("rhdg,kh,s->rksdhg", turned, head_identity(kv_heads), key_slot)
    return spread.astype(jnp.bfloat16).reshape(
        row_count, kv_heads * 2 * head_width, kv_heads * group_size
    )


def part_scores(query_block, table, first_position, lengths, cache_page_store, head_width):
    row_count = query_block.shape[0]
    cached_entries = cache_page_store[table].reshape(row_count, -1, cache_page_store.shape[-1])
    score_scale = 1.0 / math.sqrt(head_width)
    scores = (
        jnp.einsum("rlc,rcq->rql", cached_entries, query_block, preferred_element_type=jnp.float32)
        * score_scale
    )
    positions = first_position + jnp.arange(scores.shape[-1])
    is_live = positions[None, :] < lengths[:, None]
    scores = jnp.where(is_live[:, None, :], scores, -jnp.inf)
    return (cached_entries, scores)


def attend_cache(
    query_rows, new_keys, new_values, lengths, local_table, cache_page_store, sink_logits
):
    row_count, kv_heads, group_size, head_width = query_rows.shape
    score_scale = 1.0 / math.sqrt(head_width)
    query_block = spread_queries(query_rows)
    short_cached, short_scores = part_scores(
        query_block, local_table[:, :SHORT_PAGES], 0, lengths, cache_page_store, head_width
    )
    long_count = row_count // 4
    is_long = lengths > SHORT_MAX
    long_rows = jnp.nonzero(is_long, size=long_count, fill_value=0)[0].astype(jnp.int32)
    long_valid = jnp.arange(long_count) < jnp.sum(is_long.astype(jnp.int32))
    long_lengths = jnp.where(long_valid, lengths[long_rows], 0)
    long_cached, long_scores = part_scores(
        query_block[long_rows],
        local_table[long_rows, SHORT_PAGES:],
        SHORT_PAGES * PAGE_POSITIONS,
        long_lengths,
        cache_page_store,
        head_width,
    )
    own_score = (
        jnp.einsum(
            "rhgd,rhd->rhg", query_rows, new_keys, preferred_element_type=jnp.float32
        ).reshape(row_count, -1)
        * score_scale
    )
    largest = jnp.maximum(jnp.maximum(jnp.max(short_scores, axis=-1), own_score), sink_logits[None])
    largest = largest.at[long_rows].max(jnp.max(long_scores, axis=-1))
    long_largest = largest[long_rows]
    short_weight = jnp.exp(short_scores - largest[..., None])
    long_weight = jnp.exp(long_scores - long_largest[..., None])
    own_weight = jnp.exp(own_score - largest)
    denominator = jnp.sum(short_weight, axis=-1) + own_weight + jnp.exp(sink_logits[None] - largest)
    denominator = denominator.at[long_rows].add(jnp.sum(long_weight, axis=-1))
    long_denominator = denominator[long_rows]
    short_share = (short_weight / denominator[..., None]).astype(jnp.bfloat16)
    long_share = (long_weight / long_denominator[..., None]).astype(jnp.bfloat16)
    own_share = (own_weight / denominator).astype(jnp.bfloat16)
    wide_mixture = jnp.einsum(
        "rql,rlc->rqc", short_share, short_cached, preferred_element_type=jnp.float32
    )
    long_mixture = jnp.einsum(
        "rql,rlc->rqc", long_share, long_cached, preferred_element_type=jnp.float32
    )
    wide_mixture = wide_mixture.at[long_rows].add(long_mixture)
    wide_mixture = wide_mixture.reshape(row_count, kv_heads, group_size, kv_heads, 2, head_width)
    value_slot = (jnp.arange(2) == 1).astype(jnp.float32)
    mixture = jnp.einsum("rhgksd,hk,s->rhgd", wide_mixture, head_identity(kv_heads), value_slot)
    own_part = own_share.astype(jnp.float32).reshape(row_count, kv_heads, group_size)
    mixture = mixture + own_part[..., None] * new_values.astype(jnp.float32)[:, :, None, :]
    return mixture.astype(jnp.bfloat16).reshape(row_count, -1)


def expert_block(received, expand_local, expand_local_bias, reduce_local):
    sources, item_count, model_width = received.shape
    flattened = received.reshape(sources * item_count, model_width)
    pre_activation = (
        jnp.dot(flattened, expand_local, preferred_element_type=jnp.float32) + expand_local_bias
    )
    gate_part = jnp.minimum(pre_activation[:, 0::2], swiglu_limit)
    up_part = jnp.clip(pre_activation[:, 1::2], -swiglu_limit, swiglu_limit)
    activation = (gate_part * jax.nn.sigmoid(swiglu_alpha * gate_part) * (up_part + 1.0)).astype(
        jnp.bfloat16
    )
    return jnp.dot(activation, reduce_local, preferred_element_type=jnp.float32).reshape(
        sources, item_count, -1
    )


def shards(
    hidden_state,
    cached_length_list,
    page_table,
    paged_cache_store,
    attention_gain,
    qkv_weight,
    qkv_bias,
    sink_logit_values,
    output_weight,
    output_bias,
    expert_gain,
    router_weight,
    router_bias,
    expert_routes,
    expand_weight,
    expand_bias,
    reduce_weight,
    reduce_bias,
):
    rows_here, model_width = hidden_state.shape
    normed = normalize(hidden_state, attention_gain).astype(jnp.bfloat16)
    qkv_full, output_full = (
        lax.all_gather(qkv_weight, "req", axis=0, tiled=True),
        lax.all_gather(output_weight, "req", axis=1, tiled=True),
    )
    projected_rows = jnp.dot(normed, qkv_full, preferred_element_type=jnp.float32)
    projected_rows = (projected_rows + qkv_bias).reshape(
        rows_here, -1, QUERY_PER_KEY + 2, HEAD_SIZE
    )
    kv_heads = projected_rows.shape[1]
    query_rows = (
        apply_rotation(
            projected_rows[:, :, :QUERY_PER_KEY].reshape(
                rows_here, kv_heads * QUERY_PER_KEY, HEAD_SIZE
            ),
            cached_length_list,
        )
        .astype(jnp.bfloat16)
        .reshape(rows_here, kv_heads, QUERY_PER_KEY, HEAD_SIZE)
    )
    new_keys = apply_rotation(projected_rows[:, :, QUERY_PER_KEY], cached_length_list).astype(
        jnp.bfloat16
    )
    new_values = projected_rows[:, :, QUERY_PER_KEY + 1].astype(jnp.bfloat16)
    local_table = page_table - lax.axis_index("req") * paged_cache_store.shape[0]
    attended = attend_cache(
        query_rows,
        new_keys,
        new_values,
        cached_length_list,
        local_table,
        paged_cache_store,
        sink_logit_values,
    )
    partial_value = jnp.dot(attended, output_full, preferred_element_type=jnp.float32)
    head_total = lax.psum(partial_value.astype(jnp.bfloat16), "mdl").astype(jnp.float32)
    residual = (hidden_state.astype(jnp.float32) + head_total + output_bias).astype(jnp.bfloat16)
    expert_input = normalize(residual, expert_gain).astype(jnp.bfloat16)
    logits = jnp.dot(expert_input, router_weight, preferred_element_type=jnp.float32) + router_bias
    experts = router_weight.shape[1]
    route_count = expert_routes.shape[1]
    one_hot = expert_routes[:, :, None] == jnp.arange(experts)[None, None, :]
    chosen = jnp.sum(jnp.where(one_hot, logits[:, None, :], 0.0), axis=-1)
    gate_weights = jax.nn.softmax(chosen, axis=-1)
    capacity = max(2, 2 * rows_here * route_count // experts)
    pair_hot = one_hot.reshape(rows_here * route_count, experts).astype(jnp.int32)
    counts_before = jnp.cumsum(pair_hot, axis=0) - pair_hot
    slot_index = jnp.sum(counts_before * pair_hot, axis=1)
    target = expert_routes.reshape(-1) * capacity + slot_index
    placement = target[:, None] == jnp.arange(experts * capacity)[None, :]
    repeated = jnp.repeat(expert_input, route_count, axis=0)
    outgoing = jnp.einsum(
        "pc,pd->cd", placement.astype(jnp.bfloat16), repeated, preferred_element_type=jnp.float32
    )
    outgoing = outgoing.astype(jnp.bfloat16).reshape(experts, capacity, model_width)
    results = expert_block(
        lax.all_to_all(outgoing, "req", split_axis=0, concat_axis=0, tiled=True),
        expand_weight[0],
        expand_bias[0],
        reduce_weight[0],
    )
    share_width = model_width // lax.axis_size("mdl")
    offset = lax.axis_index("mdl") * share_width
    shares = lax.psum_scatter(
        results.astype(jnp.bfloat16), "mdl", scatter_dimension=2, tiled=True
    ).astype(jnp.float32)
    returned = lax.all_to_all(
        shares.astype(jnp.bfloat16), "req", split_axis=0, concat_axis=0, tiled=True
    ).astype(shares.dtype)
    picked = returned.reshape(-1, share_width)[target]
    blended = jnp.sum(
        picked.reshape(rows_here, route_count, share_width) * gate_weights[:, :, None], axis=1
    )
    bias_rows = lax.dynamic_slice_in_dim(reduce_bias, offset, share_width, 1)
    bias_term = jnp.sum(bias_rows[expert_routes] * gate_weights[:, :, None], axis=1)
    residual_share = lax.dynamic_slice_in_dim(residual, offset, share_width, 1).astype(jnp.float32)
    return (residual_share + blended + bias_term).astype(jnp.bfloat16)


def solution(mesh):
    in_specs = (
        P("req", None),
        P("req"),
        P("req", None),
        P("req", None, "mdl"),
        P(),
        P("req", "mdl"),
        P("mdl"),
        P("mdl"),
        P("mdl", "req"),
        P(),
        P(),
        P(),
        P(),
        P("req", None),
        P("req", None, "mdl"),
        P("req", "mdl"),
        P("req", "mdl", None),
        P(),
    )
    out_specs = P("req", "mdl")
    return jax.shard_map(shards, mesh=mesh, in_specs=in_specs, out_specs=out_specs, check_vma=False)
```

profile of v0, /device:TPU:32, one launch (start us, length us, event | category | flops | bytes accessed | tf_op | source)
XLA Modules:
  0.0 452.2 jit_solution(11918151416933086248)
XLA Ops:
  6.5 0.7 all-gather.7.cloned.1.call-update
  9.9 0.8 scatter_custom_fusion
  10.9 1.4 fusion.56
  12.9 1.3 gather_fusion.1
  14.9 16.5 %while.1 = (s32[]{:T(128)}, s32[32,16]{0,1:T(8,128)S(1)}, s32[8,2]{0,1:T(2,128)S(1)}, s32[8,14]{1,0:T(8,128)S(1)}, s32[]{:T(128)}, /*index=5*/s32[]{:T(128)}) while((s32[]{:T(128)}, s32[32,16]{0,1:T(8,128)S(1)}, s32[8,2]{0,1:T(2,128)S(1)}, s32[8,14]{1,0:T(8,128)S(1)}, s32[]{:T(128)}, /*index=5*/s32[]{:T(128)}) %tuple.28), condition=%wide.while_cond, body=%wide.while_body.sunk | while | flops 2 | bytes 449 | solution.py:86
  15.5 1.3 dynamic-slice.7
  17.6 1.3 dynamic-slice.7
  19.6 1.3 dynamic-slice.7
  21.7 1.3 dynamic-slice.7
  23.8 1.3 dynamic-slice.7
  25.8 1.3 dynamic-slice.7
  27.9 1.3 dynamic-slice.7
  30.0 1.3 dynamic-slice.7
  31.5 4.8 %gather_fusion = bf16[64,128,128]{2,1,0:T(8,128)(2,1)} fusion(bf16[176,128,128]{2,1,0:T(8,128)(2,1)} %param.21, s32[1024]{0:T(1024)S(1)} %pad_clamp_fusion.4), kind=kCustom, calls=%fused_computation | custom fusion | bytes 4194560 | tf_op jit(solution)/shard_map/gather | solution.py:58
  36.3 5.7 %gather_fusion.3 = bf16[112,128,128]{2,1,0:T(8,128)(2,1)} fusion(bf16[176,128,128]{2,1,0:T(8,128)(2,1)} %param.21, s32[1024]{0:T(1024)S(1)} %pad_clamp_fusion.2), kind=kCustom, calls=%fused_computation.3 | custom fusion | bytes 7340480 | tf_op jit(solution)/shard_map/gather | solution.py:58
  43.8 47.9 %all-gather.7.cloned.1.call-done = bf16[32,90,512]{2,1,0:T(8,128)(2,1)} async-done(((bf16[1,90,512]{2,1,0:T(8,128)(2,1)}), bf16[32,90,512]{2,1,0:T(8,128)(2,1)}) %all-gather.7.cloned.1.call-update) | async-done | bytes 2949136 | tf_op jit(solution)/shard_map/all_gather | solution.py:165
  91.7 4.4 reshape.625
  96.1 76.7 %all-gather.5.cloned.1.call-done = bf16[32,90,640]{2,1,0:T(8,128)(2,1)} async-done(((bf16[1,90,640]{2,1,0:T(8,128)(2,1)}), bf16[32,90,640]{2,1,0:T(8,128)(2,1)}) %all-gather.5.cloned.1.call-update) | async-done | bytes 3686416 | tf_op jit(solution)/shard_map/all_gather | solution.py:164
  172.9 4.9 %reshape.623 = bf16[2880,640]{1,0:T(8,128)(2,1)} reshape(bf16[32,90,640]{2,1,0:T(8,128)(2,1)} %all-gather.5.cloned.1.call-done) | data formatting | bytes 7372800
  177.7 2.8 convolution_add_fusion
  182.2 2.3 fusion.64
  184.6 3.2 fusion.65
  190.6 2.0 fusion.29
  192.7 2.7 fusion.21
  195.4 0.8 scatter_fusion.2
  196.8 3.5 convolution_convert_fusion.2
  200.3 62.1 %all-reduce.3.cloned.1.call-done = bf16[32,2880]{1,0:T(8,128)(2,1)} async-done(((bf16[32,2880]{1,0:T(8,128)(2,1)}), bf16[32,2880]{1,0:T(8,128)(2,1)}) %all-reduce.3.cloned.1.call-update) | async-done | bytes 184336 | tf_op jit(solution)/shard_map/psum | solution.py:197
  262.4 1.1 fusion.12
  263.6 1.1 broadcast_in_dim.57
  264.7 1.6 reshape.490
  266.3 1.8 convolution_convert_fusion.1
  268.1 2.6 copy.49
  270.6 10.1 %all-to-all-start = ((bf16[32,8,2880]{2,1,0:T(8,128)(2,1)}), bf16[32,8,2880]{2,1,0:T(8,128)(2,1)}, u32[]{:S(2)}, u32[]{:S(2)}) async-start(bf16[32,8,2880]{2,1,0:T(8,128)(2,1)} %bitcast.100), calls=%async_computation | async-start | bytes 3014656 | tf_op jit(solution)/shard_map/all_to_all | solution.py:218
  281.0 35.4 %all-to-all-done = bf16[32,8,2880]{2,1,0:T(8,128)(2,1)} async-done(((bf16[32,8,2880]{2,1,0:T(8,128)(2,1)}), bf16[32,8,2880]{2,1,0:T(8,128)(2,1)}, u32[]{:S(2)}, u32[]{:S(2)}) %all-to-all-start) | async-done | bytes 1474592 | tf_op jit(solution)/shard_map/all_to_all | solution.py:218
  316.4 4.9 %fusion.5 = f32[256,720]{0,1:T(8,128)} fusion(bf16[1,2880,720]{1,2,0:T(8,128)(2,1)} %param.32, bf16[32,8,2880]{2,1,0:T(8,128)(2,1)} %all-to-all-done, f32[720]{0:T(1024)S(1)} %reduce.1), kind=kOutput, calls=%fused_computation.22 | convolution fusion | flops 1061867520 | bytes 6361920 | tf_op jit(solution)/shard_map/dot_general | solution.py:129
  321.3 2.1 slice.39
  323.4 2.1 slice.40
  325.8 2.1 convolution_convert_fusion
  327.8 20.3 %copy.58 = bf16[32,8,2880]{1,0,2:T(8,128)(2,1)} copy(bf16[32,8,2880]{2,1,0:T(8,128)(2,1)} %convolution_convert_fusion) | data formatting | bytes 2949120
  348.2 32.7 %reshape.631 = bf16[2880,256]{1,0:T(8,128)(2,1)} reshape(bf16[2880,32,8]{2,1,0:T(8,128)(2,1)} %bitcast.94) | data formatting | bytes 2949120
  381.4 0.9 constant_dynamic-slice_fusion.1
  382.3 0.8 gather_fusion.7
  383.4 30.0 %reduce-scatter.4.cloned.1.call-done = bf16[360,256]{1,0:T(8,128)(2,1)} async-done(((bf16[2880,256]{1,0:T(8,128)(2,1)}), bf16[360,256]{1,0:T(8,128)(2,1)}) %reduce-scatter.4.cloned.1.call-update) | async-done | bytes 184336
  413.4 5.4 %reshape.632 = bf16[360,32,8]{2,1,0:T(8,128)(2,1)} reshape(bf16[360,256]{1,0:T(8,128)(2,1)} %reduce-scatter.4.cloned.1.call-done) | data formatting | bytes 368640
  418.8 4.5 copy.59
  423.3 10.0 %all-to-all-start.1 = ((bf16[32,8,360]{2,1,0:T(8,128)(2,1)}), bf16[32,8,360]{2,1,0:T(8,128)(2,1)S(1)}, u32[]{:S(2)}, u32[]{:S(2)}) async-start(bf16[32,8,360]{2,1,0:T(8,128)(2,1)} %copy.59), calls=%async_computation.1 | async-start | bytes 393216 | tf_op jit(solution)/shard_map/all_to_all | solution.py:228
  433.6 10.2 %all-to-all-done.1 = bf16[32,8,360]{2,1,0:T(8,128)(2,1)S(1)} async-done(((bf16[32,8,360]{2,1,0:T(8,128)(2,1)}), bf16[32,8,360]{2,1,0:T(8,128)(2,1)S(1)}, u32[]{:S(2)}, u32[]{:S(2)}) %all-to-all-start.1) | async-done | bytes 184352 | tf_op jit(solution)/shard_map/all_to_all | solution.py:228
  443.8 0.8 gather_fusion.6
  (148 shorter events, 19.8 us)
Async XLA Ops:
  6.5 319.2 %copy-start = (bf16[1,360,2880]{2,1,0:T(8,128)(2,1)S(1)}, bf16[1,360,2880]{2,1,0:T(8,128)(2,1)}, u32[]{:S(2)}) copy-start(bf16[1,360,2880]{2,1,0:T(8,128)(2,1)} %param.34) | copy-start | bytes 6220804
  6.5 85.2 %all-gather.7.cloned.1.call-start = ((), (), s32[]{:S(2)}) async-start(), calls=%async_computation.5 | async-start | bytes 3244032 | tf_op jit(solution)/shard_map/all_gather | solution.py:165
  7.3 165.6 %all-gather.5.cloned.1.call-start = ((), (), s32[]{:S(2)}) async-start(), calls=%async_computation.4 | async-start | bytes 4055040 | tf_op jit(solution)/shard_map/all_gather | solution.py:164
  8.0 254.4 %all-reduce.3.cloned.1.call-start = ((), (), s32[]{:S(2)}) async-start(), calls=%async_computation.3 | async-start | bytes 376832 | tf_op jit(solution)/shard_map/psum | solution.py:197
  36.3 5.7 %copy-start.5 = (s32[32,4]{0,1:T(4,128)S(1)}, s32[32,4]{0,1:T(4,128)}, u32[]{:S(2)}) copy-start(s32[32,4]{0,1:T(4,128)} %param.31) | copy-start | bytes 1540
  36.3 6.4 %copy-start.3 = (bf16[32,2880]{1,0:T(8,128)(2,1)S(1)}, bf16[32,2880]{1,0:T(8,128)(2,1)}, u32[]{:S(2)}) copy-start(bf16[32,2880]{1,0:T(8,128)(2,1)} %param.18) | copy-start | bytes 552964
  36.3 7.2 %copy-start.2 = (s32[32]{0:T(128)S(1)}, s32[32]{0:T(128)}, u32[]{:S(2)}) copy-start(s32[32]{0:T(128)} %param.19) | copy-start | bytes 388
  96.1 81.6 %copy-start.8 = (f32[2880]{0:T(1024)S(1)}, f32[2880]{0:T(1024)}, u32[]{:S(2)}) copy-start(f32[2880]{0:T(1024)} %param.22) | copy-start | bytes 34564
  96.1 81.6 %copy-start.9 = (f32[640]{0:T(1024)S(1)}, f32[640]{0:T(1024)}, u32[]{:S(2)}) copy-start(f32[640]{0:T(1024)} %param.24) | copy-start | bytes 7684
  180.6 4.0 copy-start.11
  195.4 67.0 %copy-start.7 = (f32[2880]{0:T(1024)S(1)}, f32[2880]{0:T(1024)}, u32[]{:S(2)}) copy-start(f32[2880]{0:T(1024)} %param.27) | copy-start | bytes 34564
  195.4 68.1 %copy-start.6 = (f32[2880]{0:T(1024)S(1)}, f32[2880]{0:T(1024)}, u32[]{:S(2)}) copy-start(f32[2880]{0:T(1024)} %param.28) | copy-start | bytes 34564
  268.1 12.9 %copy-start.10 = (f32[1,720]{1,0:T(1,128)S(1)}, f32[1,720]{1,0:T(1,128)}, u32[]{:S(2)}) copy-start(f32[1,720]{1,0:T(1,128)} %param.33) | copy-start | bytes 8644
  270.6 45.8 %all-to-all-start = ((bf16[32,8,2880]{2,1,0:T(8,128)(2,1)}), bf16[32,8,2880]{2,1,0:T(8,128)(2,1)}, u32[]{:S(2)}, u32[]{:S(2)}) async-start(bf16[32,8,2880]{2,1,0:T(8,128)(2,1)} %bitcast.100), calls=%async_computation | async-start | bytes 3014656 | tf_op jit(solution)/shard_map/all_to_all | solution.py:218
  280.7 132.7 %reduce-scatter.4.cloned.1.call-start = ((), (), s32[]{:S(2)}) async-start(), calls=%async_computation.6 | async-start | bytes 1658880
  380.9 2.2 copy-start.4
  380.9 2.2 copy-start.12
  418.8 26.9 %copy-start.1 = (bf16[1,360,2880]{2,1,0:T(8,128)(2,1)S(1)}, bf16[1,360,2880]{2,1,0:T(8,128)(2,1)}, u32[]{:S(2)}) copy-start(bf16[1,360,2880]{2,1,0:T(8,128)(2,1)} %param.34) | copy-start | bytes 6220804
  423.3 20.5 %all-to-all-start.1 = ((bf16[32,8,360]{2,1,0:T(8,128)(2,1)}), bf16[32,8,360]{2,1,0:T(8,128)(2,1)S(1)}, u32[]{:S(2)}, u32[]{:S(2)}) async-start(bf16[32,8,360]{2,1,0:T(8,128)(2,1)} %copy.59), calls=%async_computation.1 | async-start | bytes 393216 | tf_op jit(solution)/shard_map/all_to_all | solution.py:228
Sparse Core Ops, SparseCore 0:
  9.9 81.7 all-gather.6
  94.3 78.5 all-gather.4
  200.4 61.9 all-reduce.2
  381.1 32.2 reduce-scatter.3
where the time goes:
time: 454 us; the launch traced here: 452 us
  waiting for transfers between devices  264 us (58%)
  local copies, waits for them, and re-layouts  116 us (26%)
  matrix products  25.9 us (6%)
  starting transfers between devices  20.4 us (4%)
  between operations  13.7 us (3%)
  other arithmetic  12.6 us (3%)
    all_gather x1, waiting for transfers between devices, shards(): lax.all_gather(qkv_weight, 'req', axis=0, tiled=True)  76.7 us
    unnamed x33, local copies, waits for them, and re-layouts  72.4 us
    psum x1, waiting for transfers between devices, shards(): lax.psum(partial_value.astype(jnp.bfloat16), 'mdl').astype(jnp.float32)  62.1 us
    all_gather x1, waiting for transfers between devices, shards(): lax.all_gather(output_weight, 'req', axis=1, tiled=True)  47.9 us
    all_to_all x1, waiting for transfers between devices, shards(): lax.all_to_all(outgoing, 'req', split_axis=0, concat_axis=0, tiled=True)  35.4 us
    unnamed x5, waiting for transfers between devices  31.5 us
    gather x40, local copies, waits for them, and re-layouts  16.5 us
    gather x2, local copies, waits for them, and re-layouts, part_scores(): cache_page_store[table].reshape(row_count, -1, cache_page_store.shape[-1])  10.5 us
  transfers between devices with their start and end apart: 6, of which 6 were waited for; matrix products, arithmetic and copies ran while one was open for 9% of the time, Pallas kernels for 0%

commit v1 on v0

--- a/solution.py
+++ b/solution.py
@@ -160,8 +160,14 @@
 ):
     rows_here, model_width = hidden_state.shape
     normed = normalize(hidden_state, attention_gain).astype(jnp.bfloat16)
+    draft_waves_all = lambda local_x, axis_name: jnp.concatenate(
+        lax.all_to_all(
+            jnp.stack([local_x for _ in range(lax.axis_size(axis_name))], axis=0), axis_name, 0, 0
+        ),
+        0,
+    )
     qkv_full, output_full = (
-        lax.all_gather(qkv_weight, "req", axis=0, tiled=True),
+        draft_waves_all(qkv_weight, "req"),
         lax.all_gather(output_weight, "req", axis=1, tiled=True),
     )
     projected_rows = jnp.dot(normed, qkv_full, preferred_element_type=jnp.float32)

time: 454 us -> 419 us (0.923)
  waiting for transfers between devices: 264 us -> 216 us
  starting transfers between devices: 20.4 us -> 31.8 us
    all_gather x1 -> x0, waiting for transfers between devices: 76.7 us -> none  [shards(): lax.all_gather(qkv_weight, 'req', axis=0, tiled=True)]
    all_gather x1, waiting for transfers between devices: 47.9 us -> 76.1 us  [shards(): lax.all_gather(output_weight, 'req', axis=1, tiled=True)]
    all_to_all x0 -> x1, starting transfers between devices: none -> 11.4 us  [shards(): lax.all_to_all(jnp.stack([local_x for _ in range(lax.axis_size(axis_name)...]
    unnamed x33 -> x32, local copies, waits for them, and re-layouts: 72.4 us -> 67.4 us
    reshape x1 -> x2, local copies, waits for them, and re-layouts: 0.09 us -> 4.97 us  [the longest x1 4.88 us: shards(): jnp.concatenate(lax.all_to_all(jnp.stack([local_x for _ in range(lax.axis...]
    unnamed x5 -> x4, waiting for transfers between devices: 31.5 us -> 30.7 us
  transfers between devices with their start and end apart: 6 -> 6, of which waited for: 6 -> 5; matrix products, arithmetic and copies ran while one was open for 9% -> 10% of each run, Pallas kernels for 0% -> 0%
where the time goes in v1:
time: 419 us; the launch traced here: 417 us
  waiting for transfers between devices  216 us (52%)
  local copies, waits for them, and re-layouts  119 us (28%)
  starting transfers between devices  31.8 us (8%)
  matrix products  25.9 us (6%)
  between operations  13.7 us (3%)
  other arithmetic  10.6 us (3%)
    all_gather x1, waiting for transfers between devices, shards(): lax.all_gather(output_weight, 'req', axis=1, tiled=True)  76.1 us
    unnamed x32, local copies, waits for them, and re-layouts  67.4 us
    psum x1, waiting for transfers between devices, shards(): lax.psum(partial_value.astype(jnp.bfloat16), 'mdl').astype(jnp.float32)  63.7 us
    all_to_all x1, waiting for transfers between devices, shards(): lax.all_to_all(outgoing, 'req', split_axis=0, concat_axis=0, tiled=True)  35.4 us
    unnamed x4, waiting for transfers between devices  30.7 us
    gather x40, local copies, waits for them, and re-layouts  16.8 us
    all_to_all x1, starting transfers between devices, shards(): lax.all_to_all(jnp.stack([local_x for _ in range(lax.axis_size(axis_name)...  11.4 us
    gather x2, local copies, waits for them, and re-layouts, part_scores(): cache_page_store[table].reshape(row_count, -1, cache_page_store.shape[-1])  10.5 us
  transfers between devices with their start and end apart: 6, of which 5 were waited for; matrix products, arithmetic and copies ran while one was open for 10% of the time, Pallas kernels for 0%

profile of v1, /device:TPU:32, one launch (start us, length us, event | category | flops | bytes accessed | tf_op | source)
XLA Modules:
  0.0 416.7 jit_solution(7398898075220866958)
XLA Ops:
  6.5 3.3 stack.2
  9.8 11.4 %all-to-all-start = ((bf16[32,90,640]{2,1,0:T(8,128)(2,1)}), bf16[32,90,640]{2,1,0:T(8,128)(2,1)}, u32[]{:S(2)}, u32[]{:S(2)}) async-start(bf16[32,90,640]{2,1,0:T(8,128)(2,1)} %stack.2), calls=%async_computation | async-start | bytes 7864320 | tf_op jit(solution)/shard_map/all_to_all | solution.py:164
  21.2 0.7 all-gather.3.cloned.1.call-update
  22.5 0.8 scatter_custom_fusion
  26.1 16.9 %while.1 = (s32[]{:T(128)}, s32[32,16]{0,1:T(8,128)S(1)}, s32[8,2]{0,1:T(2,128)S(1)}, s32[8,14]{1,0:T(8,128)S(1)}, s32[]{:T(128)}, /*index=5*/s32[]{:T(128)}) while((s32[]{:T(128)}, s32[32,16]{0,1:T(8,128)S(1)}, s32[8,2]{0,1:T(2,128)S(1)}, s32[8,14]{1,0:T(8,128)S(1)}, s32[]{:T(128)}, /*index=5*/s32[]{:T(128)}) %tuple.28), condition=%wide.while_cond, body=%wide.while_body.sunk | while | flops 2 | bytes 449 | solution.py:86
  26.7 1.3 dynamic-slice.7
  28.8 1.3 dynamic-slice.7
  30.9 1.3 dynamic-slice.7
  33.1 1.3 dynamic-slice.7
  35.2 1.3 dynamic-slice.7
  37.3 1.3 dynamic-slice.7
  39.4 1.3 dynamic-slice.7
  41.5 1.3 dynamic-slice.7
  43.0 4.8 %gather_fusion = bf16[64,128,128]{2,1,0:T(8,128)(2,1)} fusion(bf16[176,128,128]{2,1,0:T(8,128)(2,1)} %param.21, s32[1024]{0:T(1024)S(1)} %pad_clamp_fusion.4), kind=kCustom, calls=%fused_computation | custom fusion | bytes 4194560 | tf_op jit(solution)/shard_map/gather | solution.py:58
  47.9 5.7 %gather_fusion.3 = bf16[112,128,128]{2,1,0:T(8,128)(2,1)} fusion(bf16[176,128,128]{2,1,0:T(8,128)(2,1)} %param.21, s32[1024]{0:T(1024)S(1)} %pad_clamp_fusion.2), kind=kCustom, calls=%fused_computation.3 | custom fusion | bytes 7340480 | tf_op jit(solution)/shard_map/gather | solution.py:58
  55.4 76.1 %all-gather.3.cloned.1.call-done = bf16[32,90,512]{2,1,0:T(8,128)(2,1)} async-done(((bf16[1,90,512]{2,1,0:T(8,128)(2,1)}), bf16[32,90,512]{2,1,0:T(8,128)(2,1)}) %all-gather.3.cloned.1.call-update) | async-done | bytes 2949136 | tf_op jit(solution)/shard_map/all_gather | solution.py:171
  131.5 4.5 %reshape.629 = bf16[2880,512]{1,0:T(8,128)(2,1)} reshape(bf16[32,90,512]{2,1,0:T(8,128)(2,1)} %all-gather.3.cloned.1.call-done) | data formatting | bytes 5898240
  136.0 4.9 %reshape.484 = bf16[2880,640]{1,0:T(8,128)(2,1)} reshape(bf16[32,90,640]{2,1,0:T(8,128)(2,1)} %all-to-all-done) | data formatting | bytes 7372800 | tf_op jit(solution)/shard_map/reshape | solution.py:163
  140.9 2.8 convolution_add_fusion
  145.4 2.3 fusion.64
  147.7 3.2 fusion.65
  153.7 2.0 fusion.29
  155.8 2.7 fusion.21
  158.5 0.8 scatter_fusion.2
  159.9 3.5 convolution_convert_fusion.2
  163.4 63.7 %all-reduce.3.cloned.1.call-done = bf16[32,2880]{1,0:T(8,128)(2,1)} async-done(((bf16[32,2880]{1,0:T(8,128)(2,1)}), bf16[32,2880]{1,0:T(8,128)(2,1)}) %all-reduce.3.cloned.1.call-update) | async-done | bytes 184336 | tf_op jit(solution)/shard_map/psum | solution.py:203
  227.1 1.1 fusion.12
  228.3 1.1 broadcast_in_dim.57
  229.4 1.6 reshape.496
  231.0 1.8 convolution_convert_fusion.1
  232.7 2.6 copy.49
  235.3 10.1 %all-to-all-start.1 = ((bf16[32,8,2880]{2,1,0:T(8,128)(2,1)}), bf16[32,8,2880]{2,1,0:T(8,128)(2,1)}, u32[]{:S(2)}, u32[]{:S(2)}) async-start(bf16[32,8,2880]{2,1,0:T(8,128)(2,1)} %bitcast.99), calls=%async_computation.1 | async-start | bytes 3014656 | tf_op jit(solution)/shard_map/all_to_all | solution.py:224
  245.7 35.4 %all-to-all-done.1 = bf16[32,8,2880]{2,1,0:T(8,128)(2,1)} async-done(((bf16[32,8,2880]{2,1,0:T(8,128)(2,1)}), bf16[32,8,2880]{2,1,0:T(8,128)(2,1)}, u32[]{:S(2)}, u32[]{:S(2)}) %all-to-all-start.1) | async-done | bytes 1474592 | tf_op jit(solution)/shard_map/all_to_all | solution.py:224
  281.1 4.9 %fusion.5 = f32[256,720]{0,1:T(8,128)} fusion(bf16[1,2880,720]{1,2,0:T(8,128)(2,1)} %param.32, bf16[32,8,2880]{2,1,0:T(8,128)(2,1)} %all-to-all-done.1, f32[720]{0:T(1024)S(1)} %reduce.1), kind=kOutput, calls=%fused_computation.22 | convolution fusion | flops 1061867520 | bytes 6361920 | tf_op jit(solution)/shard_map/dot_general | solution.py:129
  286.0 2.1 slice.39
  288.1 2.1 slice.40
  290.5 2.1 convolution_convert_fusion
  292.6 20.3 %copy.58 = bf16[32,8,2880]{1,0,2:T(8,128)(2,1)} copy(bf16[32,8,2880]{2,1,0:T(8,128)(2,1)} %convolution_convert_fusion) | data formatting | bytes 2949120
  312.9 32.7 %reshape.635 = bf16[2880,256]{1,0:T(8,128)(2,1)} reshape(bf16[2880,32,8]{2,1,0:T(8,128)(2,1)} %bitcast.93) | data formatting | bytes 2949120
  346.1 0.9 constant_dynamic-slice_fusion.1
  347.0 0.8 gather_fusion.7
  348.1 30.0 %reduce-scatter.4.cloned.1.call-done = bf16[360,256]{1,0:T(8,128)(2,1)} async-done(((bf16[2880,256]{1,0:T(8,128)(2,1)}), bf16[360,256]{1,0:T(8,128)(2,1)}) %reduce-scatter.4.cloned.1.call-update) | async-done | bytes 184336
  378.1 5.4 %reshape.636 = bf16[360,32,8]{2,1,0:T(8,128)(2,1)} reshape(bf16[360,256]{1,0:T(8,128)(2,1)} %reduce-scatter.4.cloned.1.call-done) | data formatting | bytes 368640
  383.4 4.3 %copy.59 = bf16[32,8,360]{2,1,0:T(8,128)(2,1)} copy(bf16[32,8,360]{1,0,2:T(8,128)(2,1)} %bitcast.98) | data formatting | bytes 368640
  387.8 10.1 %all-to-all-start.2 = ((bf16[32,8,360]{2,1,0:T(8,128)(2,1)}), bf16[32,8,360]{2,1,0:T(8,128)(2,1)S(1)}, u32[]{:S(2)}, u32[]{:S(2)}) async-start(bf16[32,8,360]{2,1,0:T(8,128)(2,1)} %copy.59), calls=%async_computation.2 | async-start | bytes 393216 | tf_op jit(solution)/shard_map/all_to_all | solution.py:234
  398.2 10.2 %all-to-all-done.2 = bf16[32,8,360]{2,1,0:T(8,128)(2,1)S(1)} async-done(((bf16[32,8,360]{2,1,0:T(8,128)(2,1)}), bf16[32,8,360]{2,1,0:T(8,128)(2,1)S(1)}, u32[]{:S(2)}, u32[]{:S(2)}) %all-to-all-start.2) | async-done | bytes 184352 | tf_op jit(solution)/shard_map/all_to_all | solution.py:234
  408.4 0.8 gather_fusion.6
  409.5 0.7 add_convert_fusion.2
  (148 shorter events, 18.5 us)
Async XLA Ops:
  6.5 283.9 %copy-start = (bf16[1,360,2880]{2,1,0:T(8,128)(2,1)S(1)}, bf16[1,360,2880]{2,1,0:T(8,128)(2,1)}, u32[]{:S(2)}) copy-start(bf16[1,360,2880]{2,1,0:T(8,128)(2,1)} %param.34) | copy-start | bytes 6220804
  9.8 12.2 %copy-start.8 = (s32[32,16]{0,1:T(8,128)S(1)}, s32[32,16]{0,1:T(8,128)}, u32[]{:S(2)}) copy-start(s32[32,16]{0,1:T(8,128)} %param.20) | copy-start | bytes 6148
  9.8 12.4 %copy-start.1 = (s32[32]{0:T(128)S(1)}, s32[32]{0:T(128)}, u32[]{:S(2)}) copy-start(s32[32]{0:T(128)} %param.19) | copy-start | bytes 388
  9.8 126.2 %all-to-all-start = ((bf16[32,90,640]{2,1,0:T(8,128)(2,1)}), bf16[32,90,640]{2,1,0:T(8,128)(2,1)}, u32[]{:S(2)}, u32[]{:S(2)}) async-start(bf16[32,90,640]{2,1,0:T(8,128)(2,1)} %stack.2), calls=%async_computation | async-start | bytes 7864320 | tf_op jit(solution)/shard_map/all_to_all | solution.py:164
  21.2 110.3 %all-gather.3.cloned.1.call-start = ((), (), s32[]{:S(2)}) async-start(), calls=%async_computation.5 | async-start | bytes 3244032 | tf_op jit(solution)/shard_map/all_gather | solution.py:171
  21.9 205.2 %all-reduce.3.cloned.1.call-start = ((), (), s32[]{:S(2)}) async-start(), calls=%async_computation.4 | async-start | bytes 376832 | tf_op jit(solution)/shard_map/psum | solution.py:203
  47.9 5.7 %copy-start.4 = (s32[32,4]{0,1:T(4,128)S(1)}, s32[32,4]{0,1:T(4,128)}, u32[]{:S(2)}) copy-start(s32[32,4]{0,1:T(4,128)} %param.31) | copy-start | bytes 1540
  47.9 6.4 %copy-start.2 = (bf16[32,2880]{1,0:T(8,128)(2,1)S(1)}, bf16[32,2880]{1,0:T(8,128)(2,1)}, u32[]{:S(2)}) copy-start(bf16[32,2880]{1,0:T(8,128)(2,1)} %param.18) | copy-start | bytes 552964
  136.0 4.9 %copy-start.7 = (f32[2880]{0:T(1024)S(1)}, f32[2880]{0:T(1024)}, u32[]{:S(2)}) copy-start(f32[2880]{0:T(1024)} %param.22) | copy-start | bytes 34564
  136.0 4.9 %copy-start.9 = (f32[640]{0:T(1024)S(1)}, f32[640]{0:T(1024)}, u32[]{:S(2)}) copy-start(f32[640]{0:T(1024)} %param.24) | copy-start | bytes 7684
  143.7 4.0 copy-start.11
  158.5 68.6 %copy-start.6 = (f32[2880]{0:T(1024)S(1)}, f32[2880]{0:T(1024)}, u32[]{:S(2)}) copy-start(f32[2880]{0:T(1024)} %param.27) | copy-start | bytes 34564
  158.5 69.7 %copy-start.5 = (f32[2880]{0:T(1024)S(1)}, f32[2880]{0:T(1024)}, u32[]{:S(2)}) copy-start(f32[2880]{0:T(1024)} %param.28) | copy-start | bytes 34564
  232.7 12.9 %copy-start.10 = (f32[1,720]{1,0:T(1,128)S(1)}, f32[1,720]{1,0:T(1,128)}, u32[]{:S(2)}) copy-start(f32[1,720]{1,0:T(1,128)} %param.33) | copy-start | bytes 8644
  235.3 45.8 %all-to-all-start.1 = ((bf16[32,8,2880]{2,1,0:T(8,128)(2,1)}), bf16[32,8,2880]{2,1,0:T(8,128)(2,1)}, u32[]{:S(2)}, u32[]{:S(2)}) async-start(bf16[32,8,2880]{2,1,0:T(8,128)(2,1)} %bitcast.99), calls=%async_computation.1 | async-start | bytes 3014656 | tf_op jit(solution)/shard_map/all_to_all | solution.py:224
  245.4 132.7 %reduce-scatter.4.cloned.1.call-start = ((), (), s32[]{:S(2)}) async-start(), calls=%async_computation.6 | async-start | bytes 1658880
  345.6 2.2 copy-start.3
  345.6 2.2 copy-start.12
  387.8 20.6 %all-to-all-start.2 = ((bf16[32,8,360]{2,1,0:T(8,128)(2,1)}), bf16[32,8,360]{2,1,0:T(8,128)(2,1)S(1)}, u32[]{:S(2)}, u32[]{:S(2)}) async-start(bf16[32,8,360]{2,1,0:T(8,128)(2,1)} %copy.59), calls=%async_computation.2 | async-start | bytes 393216 | tf_op jit(solution)/shard_map/all_to_all | solution.py:234
Sparse Core Ops, SparseCore 0:
  24.6 106.8 all-gather.2
  163.5 63.5 all-reduce.2
  345.8 32.2 reduce-scatter.3
